TPU v7x, 256 devices: a whole 4x4x8 slice. The times are simulated.
256 devices in a mesh: outer: 8 (over z), inner: 32 (over x, y, core).
Axes of the slice: x: 4, y: 4, z: 8, core: 2. Of those that a mesh axis runs over, the one named last changes fastest.
Arguments:
- normals: bfloat16 [1024, 512, 512], P('outer', 'inner'), may hold values from -6 to 6
- states: bfloat16 [1024, 512], P('outer'), may hold values from -0.29882812 to 0.29882812
- loadings: bfloat16 [2048, 512], replicated, may hold values from -6 to 6
- strikes: float32 [2048], replicated, may hold values from -6 to 6
- hedge: float32 [2048], replicated, may hold values from -384 to 384
- sigma: float32 [512], replicated, may hold values from 0.02 to 0.1
- tail: int32 [256], replicated, may hold values from 0 to 1023, as said below
Outputs:
- grad: float32 [2048, 512], P(('outer', 'inner'))
Inputs may be any that keep to these rules, and one draw needn't show every extreme that they name: Increasing and distinct. Group g holds nodes g * 128 to (g + 1) * 128 - 1; at most 80 tail indices fall into one group, and some group holds exactly 80.
All inputs are finite; a program needn't handle non-finite values.
Results may differ from a plain program's by a relative error of at most 0.00057.
Values may be sent and summed in bfloat16 or wider, within the bound.
A program may use at most 64 MiB of HBM per device.

v0:
```python
import jax
import jax.numpy as jnp
from jax import lax
from jax.sharding import Mesh
from jax.sharding import PartitionSpec as P

CAP = 80
INNER = ("inner_0", "inner_1", "inner_2")
OUTER_INNER = ("outer", "inner_0", "inner_1", "inner_2")


EPSILON = 1e-06


def cut_along(value, dim, count):
    dims = value.shape
    blocks = value.reshape(*dims[:dim], count, dims[dim] // count, *dims[dim + 1 :])
    return jnp.moveaxis(blocks, dim, 0)


def sum_at_owner(value, axis, dim):
    count = lax.axis_size(axis)
    blocks = lax.all_to_all(cut_along(value, dim, count), axis, 0, 0, tiled=True)
    return jnp.sum(blocks, axis=0)


def rows_for(lines, count):
    spare = -len(lines) % count
    return jnp.pad(lines, [(0, spare)] + [(0, 0)] * (lines.ndim - 1))


def joined_along(blocks, dim):
    blocks = jnp.moveaxis(blocks, 0, dim)
    dims = blocks.shape
    return blocks.reshape(*dims[:dim], dims[dim] * dims[dim + 1], *dims[dim + 2 :])


def copy_for_each(value, axis):
    count = lax.axis_size(axis)
    return lax.all_to_all(
        jnp.broadcast_to(value[None], (count, *value.shape)), axis, 0, 0, tiled=True
    )


def collect(value, axis, dim):
    return joined_along(copy_for_each(value, axis), dim)


def nested_sum(value, axes):
    own = sum_at_owner(rows_for(value, lax.axis_size(axes)), axes, 0)
    whole = collect(own, axes, 0)
    return whole[: len(value)].reshape(value.shape)


def packed_total(arrays, axis):
    flat, at, outs = (jnp.concatenate([a.reshape(-1) for a in arrays]), 0, [])
    so_far = nested_sum(flat, axis)
    for a in arrays:
        outs.append(so_far[at : at + a.size].reshape(a.shape))
        at += a.size
    return tuple(outs)


def sum_by_axis(value, axes, dim):
    far, near = axes
    own = sum_at_owner(cut_along(value, dim, lax.axis_size(far)), near, dim + 1)
    return jnp.sum(lax.all_to_all(own, far, 0, 0, tiled=True), axis=0)


def moments(values, paths):
    sums = jnp.sum(values, axis=1)
    squares = jnp.sum(values * values, axis=1)
    sums, squares = packed_total((sums, squares), INNER)
    center = sums / paths
    spread = squares / paths - center * center
    return ((values - center[:, None, :]) * lax.rsqrt(spread + EPSILON)[:, None, :]).astype(
        jnp.bfloat16
    )


def block_nodes(slots, per_node):
    limit = max(1, min(slots, 1024 // per_node))
    for count in range(limit, 0, -1):
        if slots % count == 0:
            return count
    return 1


def body(normals, states, loadings, strikes, hedge, sigma, tail):
    group = lax.axis_index("outer")
    node_count, per_node, factors_n = normals.shape
    tail_count = tail.shape[0]
    owner = tail // node_count
    flat = normals.reshape(node_count, per_node * factors_n)
    first = jnp.sum((tail < group * node_count).astype(jnp.int32))
    places = first + jnp.arange(CAP, dtype=jnp.int32)
    safe = jnp.clip(places, 0, tail_count - 1)
    valid = ((places < tail_count) & (owner[safe] == group)).astype(jnp.float32)
    local = jnp.clip(tail[safe] - group * node_count, 0, node_count - 1)
    chosen = jnp.take(flat, local, axis=0)
    levels = jnp.take(states, local, axis=0)
    paths = per_node * lax.axis_size(INNER)
    values = chosen.reshape(CAP, per_node, factors_n).astype(jnp.float32)
    scaled = moments(values, paths)
    slots = CAP
    width = block_nodes(slots, per_node)
    blocks = slots // width
    scaled_blocks = scaled.reshape(blocks, width, per_node, factors_n)
    level_blocks = levels.reshape(blocks, width, factors_n)
    valid_blocks = valid.reshape(blocks, width)

    def block(total, items):
        scaled_part, level_part, valid_part = items
        mixed = (
            level_part.astype(jnp.float32)[:, None, :] + sigma * scaled_part.astype(jnp.float32)
        ).astype(jnp.bfloat16)
        mixed = mixed.reshape(width * per_node, factors_n)
        level = (
            lax.dot_general(
                mixed, loadings, (((1,), (1,)), ((), ())), preferred_element_type=jnp.float32
            )
            - strikes
        )
        live = jnp.repeat(valid_part, per_node)
        weight = (hedge * jax.nn.sigmoid(level) * live[:, None]).astype(jnp.bfloat16)
        cross = lax.dot_general(
            weight,
            scaled_part.reshape(width * per_node, factors_n),
            (((0,), (0,)), ((), ())),
            preferred_element_type=jnp.float32,
        )
        return (total + cross, None)

    total, unused = lax.scan(
        block,
        jnp.zeros((loadings.shape[0], factors_n), jnp.float32),
        (scaled_blocks, level_blocks, valid_blocks),
    )
    owned = sum_by_axis(total, (("outer", "inner_0"), ("inner_1", "inner_2")), 0)
    rows = owned.shape[0]
    position = lax.axis_index("outer") * lax.axis_size(INNER) + lax.axis_index(INNER)
    own_loadings = lax.dynamic_slice_in_dim(loadings, position * rows, rows, 0).astype(jnp.float32)
    return own_loadings * owned / (tail_count * paths)


def solution(mesh):
    torus = Mesh(
        mesh.devices.reshape(mesh.shape["outer"], 4, 4, 2),
        ("outer", "inner_0", "inner_1", "inner_2"),
    )
    in_specs = (P("outer", INNER, None), P("outer", None), P(), P(), P(), P(), P())
    out_specs = P(OUTER_INNER, None)
    return jax.shard_map(body, mesh=torus, in_specs=in_specs, out_specs=out_specs, check_vma=False)
```

profile of v0, /device:TPU:1, one launch (start us, length us, event | category | flops | bytes accessed | tf_op | source)
XLA Modules:
  0.0 146.6 jit_solution(4976120640056430720)
XLA Ops:
  0.0 0.0 copy-start
  0.0 1.4 and_select_fusion
  1.4 0.7 fusion.7
  2.0 1.6 %gather_fusion = s32[80]{0:T(128)S(1)} fusion(s32[256]{0:T(256)} %param.15, s32[1024]{0:T(1024)S(1)} %pad_clamp_fusion.1), kind=kCustom, calls=%fused_computation | custom fusion | bytes 960 | tf_op jit(solution)/shard_map/gather | solution.py:99
  3.7 0.0 copy-start.4
  3.7 0.6 copy-done.4
  4.3 3.0 %copy.10 = bf16[16,8,16,512]{3,1,2,0:T(8,128)(2,1)S(1)} copy(bf16[16,8,16,512]{3,2,1,0:T(8,128)(2,1)} %bitcast.61) | data formatting | bytes 4194304
  7.2 1.4 gather_fusion.2
  8.6 0.5 copy.11
  9.1 0.0 copy-start.1
  9.1 0.0 copy-start.5
  9.1 1.0 convert_reduce_fusion
  10.2 0.1 concatenate.8
  10.2 0.1 concatenate.9
  10.3 0.9 all_to_all.16
  11.3 8.6 %all-to-all-start = ((f32[32,1,2560]{2,1,0:T(1,128)}), f32[32,1,2560]{2,1,0:T(1,128)S(1)}, u32[]{:S(2)}, u32[]{:S(2)}) async-start(f32[32,1,2560]{2,1,0:T(1,128)} %all_to_all.16), calls=%async_computation | async-start | bytes 655360 | tf_op jit(solution)/shard_map/all_to_all | solution.py:23
  19.9 1.3 gather_fusion.3
  21.2 0.0 copy-done.5
  21.2 0.1 min.24
  21.2 0.1 eq.12
  21.3 0.7 and_convert_fusion
  22.0 7.5 %all-to-all-done = f32[32,1,2560]{2,1,0:T(1,128)S(1)} async-done(((f32[32,1,2560]{2,1,0:T(1,128)}), f32[32,1,2560]{2,1,0:T(1,128)S(1)}, u32[]{:S(2)}, u32[]{:S(2)}) %all-to-all-start) | async-done | bytes 327712 | tf_op jit(solution)/shard_map/all_to_all | solution.py:23
  29.5 0.2 reduce_sum.57
  29.7 0.9 broadcast_in_dim.51
  30.6 0.0 copy-done.1
  30.6 3.8 %all-to-all-start.1 = ((f32[32,1,2560]{2,1,0:T(1,128)}), f32[32,1,2560]{2,1,0:T(1,128)S(1)}, u32[]{:S(2)}, u32[]{:S(2)}) async-start(f32[32,1,2560]{2,1,0:T(1,128)} %broadcast_in_dim.51), calls=%async_computation.1 | async-start | bytes 655360 | tf_op jit(solution)/shard_map/all_to_all | solution.py:40
  34.5 0.0 copy-start.2
  34.5 0.0 copy-done
  34.5 0.7 gather_fusion.1
  35.2 0.0 copy-start.3
  35.3 0.0 copy-start.6
  35.3 0.0 copy-start.7
  35.3 0.1 broadcast_select_fusion
  35.4 8.6 %all-to-all-done.1 = f32[32,1,2560]{2,1,0:T(1,128)S(1)} async-done(((f32[32,1,2560]{2,1,0:T(1,128)}), f32[32,1,2560]{2,1,0:T(1,128)S(1)}, u32[]{:S(2)}, u32[]{:S(2)}) %all-to-all-start.1) | async-done | bytes 327712 | tf_op jit(solution)/shard_map/all_to_all | solution.py:40
  44.0 0.9 fusion.5
  45.0 0.0 copy-done.2
  45.0 0.5 multiply_convert_fusion.1
  45.5 0.0 copy-done.3
  45.5 0.0 copy-done.6
  45.6 0.0 copy-done.7
  45.6 16.6 %while.11 = (s32[]{:T(128)}, f32[2048,512]{1,0:T(8,128)}, f32[2048]{0:T(1024)S(1)}, bf16[2,40,512]{2,1,0:T(8,128)(2,1)S(1)}, f32[512]{0:T(512)S(1)}, /*index=5*/...) while((s32[]{:T(128)}, f32[2048,512]{1,0:T(8,128)}, ...), condition=%wide.region_5.6_spmd.clone, body=%wide.region_4.5_spmd.clone.sunk | while | flops 2696957952 | bytes 14652011 | solution.py:134
  45.6 0.1 broadcast_in_dim.68
  45.7 0.1 mul.116
  45.8 0.1 constant_dynamic-slice_fusion.3
  45.8 0.2 fusion.20
  46.0 7.2 %select_add_fusion.2 = f32[2048,512]{1,0:T(8,128)} fusion(f32[2048,512]{1,0:T(8,128)} %get-tuple-element.176, bf16[640,512]{1,0:T(8,128)(2,1)S(1)} %bitcast.57, pred[]{:T(512)S(6)} %compare.5, bf16[640,512]{1,0:T(8,128)(2,1)S(1)} %fusion.20, bf16[2048,512]{1,0:T(8,128)(2,1)} %get-tuple-element.192, f32[640]{0:T(1024)S(1)} %mul.116, ...), kind=kOutput, calls=%fused_computation.5.clone.1 | convolution fusion | flops 2695626752 | bytes 11815425 | tf_op jit(solution)/shard_map/while/body/eval_jaxpr/dot_general | solution.py:126
  53.3 0.1 broadcast_in_dim.68
  53.3 0.1 mul.116
  53.4 0.1 constant_dynamic-slice_fusion.3
  53.5 0.2 fusion.20
  53.7 8.5 %select_add_fusion.2 = f32[2048,512]{1,0:T(8,128)} fusion(f32[2048,512]{1,0:T(8,128)} %get-tuple-element.176, bf16[640,512]{1,0:T(8,128)(2,1)S(1)} %bitcast.57, pred[]{:T(512)S(6)} %compare.5, bf16[640,512]{1,0:T(8,128)(2,1)S(1)} %fusion.20, bf16[2048,512]{1,0:T(8,128)(2,1)} %get-tuple-element.192, f32[640]{0:T(1024)S(1)} %mul.116, ...), kind=kOutput, calls=%fused_computation.5.clone.1 | convolution fusion | flops 2695626752 | bytes 11815425 | tf_op jit(solution)/shard_map/while/body/eval_jaxpr/dot_general | solution.py:126
  62.1 2.8 %copy.9 = f32[8,32,8,512]{3,2,1,0:T(8,128)S(1)} copy(f32[8,32,8,512]{3,2,0,1:T(8,128)} %bitcast.60) | data formatting | bytes 8388608 | tf_op jit(solution)/shard_map/transpose | solution.py:18
  65.0 52.0 %all_to_all.25 = f32[8,32,8,512]{3,2,1,0:T(8,128)} all-to-all(f32[8,32,8,512]{3,2,1,0:T(8,128)S(1)} %copy.9), channel_id=1, replica_groups=mesh['outer'=8,'inner_0'=4,'inner_1'=4,'inner_2'=2] {'inner_1','inner_2'}, dimensions={0} | all-to-all | bytes 8388608 | tf_op jit(solution)/shard_map/all_to_all | solution.py:23
  117.0 3.5 %reduce_sum.58 = f32[32,8,512]{2,1,0:T(8,128)} reduce(f32[8,32,8,512]{3,2,1,0:T(8,128)} %all_to_all.25, f32[]{:T(128)} %constant.87.clone.1), dimensions={0}, to_apply=%region_6.7 | reduce | flops 917504 | bytes 4718596 | tf_op jit(solution)/shard_map/reduce_sum | solution.py:24
  120.5 9.4 %all-to-all-start.3 = ((f32[32,8,512]{2,1,0:T(8,128)}), f32[32,8,512]{2,1,0:T(8,128)S(1)}, u32[]{:S(2)}, u32[]{:S(2)}) async-start(f32[32,8,512]{2,1,0:T(8,128)} %reduce_sum.58), calls=%async_computation.3 | async-start | bytes 1048576 | tf_op jit(solution)/shard_map/all_to_all | solution.py:67
  129.9 15.3 %all-to-all-done.3 = f32[32,8,512]{2,1,0:T(8,128)S(1)} async-done(((f32[32,8,512]{2,1,0:T(8,128)}), f32[32,8,512]{2,1,0:T(8,128)S(1)}, u32[]{:S(2)}, u32[]{:S(2)}) %all-to-all-start.3) | async-done | bytes 524320 | tf_op jit(solution)/shard_map/all_to_all | solution.py:67
  145.3 1.3 multiply_multiply_fusion
  (16 shorter events, 0.3 us)
Async XLA Ops:
  0.0 34.5 %copy-start = (bf16[128,512]{1,0:T(8,128)(2,1)S(1)}, bf16[128,512]{1,0:T(8,128)(2,1)}, u32[]{:S(2)}) copy-start(bf16[128,512]{1,0:T(8,128)(2,1)} %param.10) | copy-start | bytes 393220
  3.7 0.6 copy-start.4
  9.1 21.5 %copy-start.1 = (bf16[10,8,16,512]{3,2,1,0:T(8,128)(2,1)}, bf16[10,8,16,512]{3,2,1,0:T(8,128)(2,1)S(1)}, u32[]{:S(2)}) copy-start(bf16[10,8,16,512]{3,2,1,0:T(8,128)(2,1)S(1)} %copy.11) | copy-start | bytes 3932164
  9.1 12.1 %copy-start.5 = (s32[80]{0:T(128)S(1)}, s32[80]{0:T(128)}, u32[]{:S(2)}) copy-start(s32[80]{0:T(128)} %copy-done.4) | copy-start | bytes 964
  11.3 18.2 %all-to-all-start = ((f32[32,1,2560]{2,1,0:T(1,128)}), f32[32,1,2560]{2,1,0:T(1,128)S(1)}, u32[]{:S(2)}, u32[]{:S(2)}) async-start(f32[32,1,2560]{2,1,0:T(1,128)} %all_to_all.16), calls=%async_computation | async-start | bytes 655360 | tf_op jit(solution)/shard_map/all_to_all | solution.py:23
  30.6 13.4 %all-to-all-start.1 = ((f32[32,1,2560]{2,1,0:T(1,128)}), f32[32,1,2560]{2,1,0:T(1,128)S(1)}, u32[]{:S(2)}, u32[]{:S(2)}) async-start(f32[32,1,2560]{2,1,0:T(1,128)} %broadcast_in_dim.51), calls=%async_computation.1 | async-start | bytes 655360 | tf_op jit(solution)/shard_map/all_to_all | solution.py:40
  34.5 10.6 %copy-start.2 = (bf16[10,8,16,512]{3,2,1,0:T(8,128)(2,1)S(1)}, bf16[10,8,16,512]{3,2,1,0:T(8,128)(2,1)}, u32[]{:S(2)}) copy-start(bf16[10,8,16,512]{3,2,1,0:T(8,128)(2,1)} %copy-done.1) | copy-start | bytes 3932164
  35.2 10.3 %copy-start.3 = (f32[512]{0:T(512)S(1)}, f32[512]{0:T(512)}, u32[]{:S(2)}) copy-start(f32[512]{0:T(512)} %param.14) | copy-start | bytes 6148
  35.3 10.3 %copy-start.6 = (f32[2048]{0:T(1024)S(1)}, f32[2048]{0:T(1024)}, u32[]{:S(2)}) copy-start(f32[2048]{0:T(1024)} %param.13) | copy-start | bytes 24580
  35.3 10.3 %copy-start.7 = (f32[2048]{0:T(1024)S(1)}, f32[2048]{0:T(1024)}, u32[]{:S(2)}) copy-start(f32[2048]{0:T(1024)} %param.12) | copy-start | bytes 24580
  120.5 24.8 %all-to-all-start.3 = ((f32[32,8,512]{2,1,0:T(8,128)}), f32[32,8,512]{2,1,0:T(8,128)S(1)}, u32[]{:S(2)}, u32[]{:S(2)}) async-start(f32[32,8,512]{2,1,0:T(8,128)} %reduce_sum.58), calls=%async_computation.3 | async-start | bytes 1048576 | tf_op jit(solution)/shard_map/all_to_all | solution.py:67
where the time goes:
time: 149 us; the launch traced here: 147 us
  blocking collectives  52 us (35%)
  waiting for transfers between devices  31.4 us (21%)
  starting transfers between devices  21.8 us (15%)
  matrix products  15.7 us (11%)
  local copies, waits for them, and re-layouts  14.5 us (10%)
  other arithmetic  10.7 us (7%)
    all_to_all x1, blocking collectives, sum_at_owner(): lax.all_to_all(cut_along(value, dim, count), axis, 0, 0, tiled=True)  52 us
    dot_general x2, matrix products, block(): lax.dot_general(weight, scaled_part.reshape(width * per_node, factors_n),...  15.7 us
    all_to_all x1, waiting for transfers between devices, sum_by_axis(): return jnp.sum(lax.all_to_all(own, far, 0, 0, tiled=True), axis=0)  15.3 us
    all_to_all x1, starting transfers between devices, sum_by_axis(): return jnp.sum(lax.all_to_all(own, far, 0, 0, tiled=True), axis=0)  9.43 us
    all_to_all x1, waiting for transfers between devices, copy_for_each(): lax.all_to_all(jnp.broadcast_to(value[None], (count, *value.shape)), axis...  8.62 us
    all_to_all x1, starting transfers between devices, sum_at_owner(): lax.all_to_all(cut_along(value, dim, count), axis, 0, 0, tiled=True)  8.58 us
    all_to_all x1, waiting for transfers between devices, sum_at_owner(): lax.all_to_all(cut_along(value, dim, count), axis, 0, 0, tiled=True)  7.5 us
    unnamed x18, local copies, waits for them, and re-layouts  4.03 us
  transfers between devices with their start and end apart: 3, of which 3 were waited for; matrix products, arithmetic and copies ran while one was open for 2% of the time, Pallas kernels for 0%

commit v1 on v0

v1 whole, which is shorter than its diff:
```python
import jax
import jax.numpy as jnp
from jax import lax
from jax.experimental import pallas as pl
from jax.experimental.pallas import tpu as pltpu
from jax.sharding import PartitionSpec as P

CAP = 80
EPSILON = 1e-06
CHUNKS = 4
BLOCKS = 5
MESH = pl.DeviceIdType.MESH
F32 = jnp.float32
BF16 = jnp.bfloat16


def place(hit):
    return jnp.where(hit, 1.0, 0.0)


def kernel(
    normals, states, loadings, strikes, hedge, sigma, tail, out,
    own, pair, load_v, states_b, states_f, strikes_v, hedge_v, sigma_v, tail_s, slot_s, live_s,
    sums, sums_in, stat, stats, half_strike, half_hedge, own_load, load_t,
    mixed, part, turned, weight, acc, sent, in_x, in_y, mid_x, mid_y, in_xy, in_yx, last, in_z,
    copy_sem, pair_sem, sum_out, sum_in, stat_out, stat_in,
    x_out, x_in, y_out, y_in, xy_out, xy_in, yx_out, yx_in, z_out, z_in,
):
    z = lax.axis_index("outer")
    me = lax.axis_index("inner")
    x, y, c = me // 8, (me // 2) % 4, me % 2
    nodes, per_node, factors = own.shape
    paths = per_node * 32
    tails = tail_s.shape[0]

    loads = [
        pltpu.make_async_copy(tail, tail_s, copy_sem.at[0]),
        pltpu.make_async_copy(normals, own, copy_sem.at[1]),
        pltpu.make_async_copy(states, states_b, copy_sem.at[2]),
        pltpu.make_async_copy(sigma, sigma_v, copy_sem.at[3]),
        pltpu.make_async_copy(strikes, strikes_v, copy_sem.at[4]),
        pltpu.make_async_copy(hedge, hedge_v, copy_sem.at[5]),
        pltpu.make_async_copy(loadings, load_v, copy_sem.at[6]),
    ]
    for item in loads:
        item.start()

    barrier = pltpu.get_barrier_semaphore()

    def greet_plane(r, carry):
        pl.semaphore_signal(
            barrier, inc=1, device_id=(z, (me + r) % 32), device_id_type=MESH
        )
        return carry

    def greet_line(r, carry):
        pl.semaphore_signal(
            barrier, inc=1, device_id=((z + r) % 8, me), device_id_type=MESH
        )
        return carry

    lax.fori_loop(1, 32, greet_plane, 0)
    lax.fori_loop(1, 8, greet_line, 0)

    loads[0].wait()
    first = jnp.int32(0)
    step = tails // 2
    while step:
        first = first + jnp.where(tail_s[first + step - 1] < z * nodes, step, 0)
        step //= 2

    def find(s, carry):
        at = jnp.minimum(first + s, tails - 1)
        node = tail_s[at] - z * nodes
        good = (first + s < tails) & (node >= 0) & (node < nodes)
        slot_s[s] = jnp.clip(node, 0, nodes - 1)
        live_s[s] = jnp.where(good, 1.0, 0.0).astype(F32)
        return carry

    lax.fori_loop(0, CAP, find, 0)
    loads[1].wait()

    def add_up(q, carry):
        for i in range(5):
            block = own[slot_s[q * 5 + i]].astype(F32)
            one = jnp.sum(block, axis=0, keepdims=True)
            two = jnp.sum(block * block, axis=0, keepdims=True)
            for h in range(2):
                for b in range(2):
                    lanes = slice(h * 256 + b * 128, h * 256 + b * 128 + 128)
                    sums[q * 2 + h, i, b : b + 1, :] = one[:, lanes]
                    sums[q * 2 + h, i, 2 + b : 3 + b, :] = two[:, lanes]
        return carry

    lax.fori_loop(0, 16, add_up, 0)
    pl.semaphore_wait(barrier, 38)

    def sum_copy(r, owner, source):
        return pltpu.make_async_remote_copy(
            src_ref=sums.at[owner], dst_ref=sums_in.at[source],
            send_sem=sum_out.at[r], recv_sem=sum_in.at[r],
            device_id=(z, owner), device_id_type=MESH,
        )

    def send_sums(r, carry):
        sum_copy(r, (me + r) % 32, me).start()
        return carry

    lax.fori_loop(1, 32, send_sums, 0)
    swap = pltpu.make_async_remote_copy(
        src_ref=own, dst_ref=pair, send_sem=pair_sem.at[0], recv_sem=pair_sem.at[1],
        device_id=(z, me + 1 - 2 * c), device_id_type=MESH,
    )
    swap.start()

    for item in loads[2:]:
        item.wait()
    states_f[...] = states_b[...].astype(F32)
    m_id = lax.broadcasted_iota(jnp.int32, (256, 256), 0)
    l_id = lax.broadcasted_iota(jnp.int32, (256, 256), 1)
    same = (m_id // 16 == l_id // 16) & (m_id % 8 == l_id % 8)
    picks = [same & ((m_id // 8) % 2 == c) & ((l_id // 8) % 2 == a) for a in range(2)]
    same_t = (m_id // 16 == l_id // 16) & (m_id % 8 == l_id % 8)
    picks_t = [same_t & ((l_id // 8) % 2 == c) & ((m_id // 8) % 2 == a) for a in range(2)]
    for source, target in ((strikes_v, half_strike), (hedge_v, half_hedge)):
        rows = source[...] * 0.5
        moved = [
            jnp.dot(rows, place(pick), precision=lax.Precision.HIGHEST, preferred_element_type=F32)
            for pick in picks
        ]
        for j in range(CHUNKS):
            target[j] = moved[0][2 * j : 2 * j + 1] + moved[1][2 * j + 1 : 2 * j + 2]
    turn = [place(pick).astype(BF16) for pick in picks_t]

    def order(j, carry):
        rows = jnp.zeros((256, factors), F32)
        for a in range(2):
            at = pl.multiple_of((2 * j + a) * 256, 256)
            rows = rows + jnp.dot(turn[a], load_v[pl.ds(at, 256), :], preferred_element_type=F32)
        own_load[j] = rows
        load_t[j] = (rows * 0.5).astype(BF16).T
        return carry

    lax.fori_loop(0, CHUNKS, order, 0)

    def wait_sums(r, carry):
        sum_copy(r, me, (me + 32 - r) % 32).wait_recv()
        return carry

    lax.fori_loop(1, 32, wait_sums, 0)

    def gather_sums(r, total):
        return total + sums_in[(me + r) % 32]

    total = lax.fori_loop(1, 32, gather_sums, sums[me])
    center = total[:, 0:2, :] / paths
    spread = total[:, 2:4, :] / paths - center * center
    stat[:, 0:2, :] = center
    stat[:, 2:4, :] = lax.rsqrt(spread + EPSILON)
    stats[me] = stat[...]

    def stat_copy(r, target, source):
        return pltpu.make_async_remote_copy(
            src_ref=stat, dst_ref=stats.at[source],
            send_sem=stat_out.at[r], recv_sem=stat_in.at[r],
            device_id=(z, target), device_id_type=MESH,
        )

    def send_stats(r, carry):
        stat_copy(r, (me + r) % 32, me).start()
        return carry

    lax.fori_loop(1, 32, send_stats, 0)
    swap.wait_recv()

    def wait_stats(r, carry):
        stat_copy(r, me, (me + 32 - r) % 32).wait_recv()
        return carry

    lax.fori_loop(1, 32, wait_stats, 0)

    def normalise(blk, carry):
        for u in range(4):
            s = blk * 4 + u
            q, i = s // 5, s % 5
            at, live = slot_s[s], live_s[s]
            state = states_f[pl.ds(at, 1), :]
            for e, source in enumerate((own, pair)):
                block = source[at]
                row = pl.multiple_of(s * 32 + e * 16, 16)
                for lane in range(4):
                    h, b = lane // 2, lane % 2
                    lanes = slice(lane * 128, lane * 128 + 128)
                    mean = stats[q * 2 + h, i, b : b + 1, :]
                    scale = stats[q * 2 + h, i, 2 + b : 3 + b, :] * live
                    scaled = ((block[:, lanes].astype(F32) - mean) * scale).astype(BF16)
                    both = state[:, lanes] + sigma_v[:, lanes] * scaled.astype(F32)
                    mixed[pl.ds(row, 16), lanes] = both.astype(BF16)
                    part[u * 32 + e * 16 : u * 32 + e * 16 + 16, lanes] = scaled
        at = pl.multiple_of((blk % 4) * 128, 128)
        turned[blk // 4, :, pl.ds(at, 128)] = part[...].T
        return carry

    lax.fori_loop(0, CAP // 4, normalise, 0)

    def weigh(j, b):
        at = b * 512 if isinstance(b, int) else pl.multiple_of(b * 512, 512)
        level = jnp.dot(mixed[pl.ds(at, 512), :], load_t[j], preferred_element_type=F32)
        size = half_hedge[j]
        return (size + size * jnp.tanh(level - half_strike[j])).astype(BF16)

    def cross(b, slot):
        return jnp.dot(turned[b], weight[slot], preferred_element_type=F32)

    def x_copy(j, r):
        px = (x + r) % 4
        return pltpu.make_async_remote_copy(
            src_ref=sent.at[j, px, :, :, pl.ds(0, 256)], dst_ref=in_x.at[j, r - 1],
            send_sem=x_out.at[j, r - 1], recv_sem=x_in.at[j, r - 1],
            device_id=(z, (px * 4 + y) * 2 + c), device_id_type=MESH,
        )

    def y_copy(j, r):
        py = (y + r) % 4
        return pltpu.make_async_remote_copy(
            src_ref=sent.at[j, :, py, :, pl.ds(256, 256)], dst_ref=in_y.at[j, r - 1],
            send_sem=y_out.at[j, r - 1], recv_sem=y_in.at[j, r - 1],
            device_id=(z, (x * 4 + py) * 2 + c), device_id_type=MESH,
        )

    def xy_copy(j, r):
        py = (y + r) % 4
        return pltpu.make_async_remote_copy(
            src_ref=mid_x.at[j, py], dst_ref=in_xy.at[j, r - 1],
            send_sem=xy_out.at[j, r - 1], recv_sem=xy_in.at[j, r - 1],
            device_id=(z, (x * 4 + py) * 2 + c), device_id_type=MESH,
        )

    def yx_copy(j, r):
        px = (x + r) % 4
        return pltpu.make_async_remote_copy(
            src_ref=mid_y.at[j, px], dst_ref=in_yx.at[j, r - 1],
            send_sem=yx_out.at[j, r - 1], recv_sem=yx_in.at[j, r - 1],
            device_id=(z, (px * 4 + y) * 2 + c), device_id_type=MESH,
        )

    def z_copy(j, a, slot):
        return pltpu.make_async_remote_copy(
            src_ref=last.at[j, a], dst_ref=in_z.at[slot],
            send_sem=z_out.at[j, a], recv_sem=z_in.at[slot],
            device_id=(2 * j + a, me), device_id_type=MESH,
        )

    def finish(j):
        rows = acc[...].astype(BF16).T
        sent[j] = rows.reshape(4, 4, 16, factors)
        for r in (2, 1, 3):
            x_copy(j, r).start()
            y_copy(j, r).start()

    def second(j):
        for r in (1, 2, 3):
            x_copy(j, r).wait_recv()
        total = sent[j, x, :, :, 0:256].astype(F32)
        for r in range(3):
            total = total + in_x[j, r].astype(F32)
        mid_x[j] = total
        for r in (1, 2, 3):
            y_copy(j, r).wait_recv()
        total = sent[j, :, y, :, 256:512].astype(F32)
        for r in range(3):
            total = total + in_y[j, r].astype(F32)
        mid_y[j] = total
        for r in (2, 1, 3):
            xy_copy(j, r).start()
            yx_copy(j, r).start()

    def third(j):
        for r in (1, 2, 3):
            xy_copy(j, r).wait_recv()
        one = mid_x[j, y]
        for r in range(3):
            one = one + in_xy[j, r]
        for r in (1, 2, 3):
            yx_copy(j, r).wait_recv()
        two = mid_y[j, x]
        for r in range(3):
            two = two + in_yx[j, r]
        for a in range(2):
            last[j, a, :, 0:256] = one[a * 8 : a * 8 + 8]
            last[j, a, :, 256:512] = two[a * 8 : a * 8 + 8]
        for a in range(2):
            @pl.when(z != 2 * j + a)
            def _():
                z_copy(j, a, (z - (2 * j + a) + 8) % 8 - 1).start()

    for j in range(CHUNKS):
        fresh = weigh(j, 0)
        if j:
            acc[...] += cross(BLOCKS - 1, (BLOCKS * j - 1) % 2)
            finish(j - 1)
        weight[(BLOCKS * j) % 2] = fresh
        acc[...] = jnp.zeros_like(acc)

        def one_block(b, carry, j=j):
            slot = (BLOCKS * j + b) % 2
            fresh = weigh(j, b)
            acc[...] += cross(b - 1, 1 - slot)
            weight[slot] = fresh
            return carry

        lax.fori_loop(1, BLOCKS, one_block, 0)
        if j >= 2:
            second(j - 2)
    acc[...] += cross(BLOCKS - 1, (BLOCKS * CHUNKS - 1) % 2)
    finish(CHUNKS - 1)
    third(0)
    second(2)
    third(1)
    second(3)
    third(2)
    third(3)

    for slot in range(7):
        z_copy(0, 0, slot).wait_recv()
    total = last[z // 2, z % 2]
    for slot in range(7):
        total = total + in_z[slot]
    at = pl.multiple_of((x * 4 + y) * 16 + (z % 2) * 8, 8)
    out[...] = own_load[z // 2, pl.ds(at, 8), :] * total / (tails * paths)

    swap.wait_send()

    def drain(r, carry):
        sum_copy(r, (me + r) % 32, me).wait_send()
        stat_copy(r, (me + r) % 32, me).wait_send()
        return carry

    lax.fori_loop(1, 32, drain, 0)
    for j in range(CHUNKS):
        for r in (1, 2, 3):
            x_copy(j, r).wait_send()
            y_copy(j, r).wait_send()
            xy_copy(j, r).wait_send()
            yx_copy(j, r).wait_send()
        for a in range(2):
            @pl.when(z != 2 * j + a)
            def _():
                z_copy(j, a, 0).wait_send()


def body(normals, states, loadings, strikes, hedge, sigma, tail):
    nodes, per_node, factors = normals.shape
    rows = CAP * per_node * 2
    dma = pltpu.SemaphoreType.DMA
    return pl.pallas_call(
        kernel,
        out_shape=jax.ShapeDtypeStruct((8, factors), F32),
        in_specs=[pl.BlockSpec(memory_space=pltpu.HBM)] * 7,
        out_specs=pl.BlockSpec(memory_space=pltpu.VMEM),
        scratch_shapes=[
            pltpu.VMEM(normals.shape, BF16),
            pltpu.VMEM(normals.shape, BF16),
            pltpu.VMEM(loadings.shape, BF16),
            pltpu.VMEM(states.shape, BF16),
            pltpu.VMEM(states.shape, F32),
            pltpu.VMEM((8, 256), F32),
            pltpu.VMEM((8, 256), F32),
            pltpu.VMEM((1, factors), F32),
            pltpu.SMEM(tail.shape, jnp.int32),
            pltpu.SMEM((CAP,), jnp.int32),
            pltpu.SMEM((CAP,), F32),
            pltpu.VMEM((32, 5, 4, 128), F32),
            pltpu.VMEM((32, 5, 4, 128), F32),
            pltpu.VMEM((5, 4, 128), F32),
            pltpu.VMEM((32, 5, 4, 128), F32),
            pltpu.VMEM((CHUNKS, 1, 256), F32),
            pltpu.VMEM((CHUNKS, 1, 256), F32),
            pltpu.VMEM((CHUNKS, 256, factors), F32),
            pltpu.VMEM((CHUNKS, factors, 256), BF16),
            pltpu.VMEM((rows, factors), BF16),
            pltpu.VMEM((128, factors), BF16),
            pltpu.VMEM((BLOCKS, factors, 512), BF16),
            pltpu.VMEM((2, 512, 256), BF16),
            pltpu.VMEM((factors, 256), F32),
            pltpu.VMEM((CHUNKS, 4, 4, 16, factors), BF16),
            pltpu.VMEM((CHUNKS, 3, 4, 16, 256), BF16),
            pltpu.VMEM((CHUNKS, 3, 4, 16, 256), BF16),
            pltpu.VMEM((CHUNKS, 4, 16, 256), F32),
            pltpu.VMEM((CHUNKS, 4, 16, 256), F32),
            pltpu.VMEM((CHUNKS, 3, 16, 256), F32),
            pltpu.VMEM((CHUNKS, 3, 16, 256), F32),
            pltpu.VMEM((CHUNKS, 2, 8, factors), F32),
            pltpu.VMEM((7, 8, factors), F32),
            dma((7,)),
            dma((2,)),
            dma((32,)),
            dma((32,)),
            dma((32,)),
            dma((32,)),
            dma((CHUNKS, 3)),
            dma((CHUNKS, 3)),
            dma((CHUNKS, 3)),
            dma((CHUNKS, 3)),
            dma((CHUNKS, 3)),
            dma((CHUNKS, 3)),
            dma((CHUNKS, 3)),
            dma((CHUNKS, 3)),
            dma((CHUNKS, 2)),
            dma((7,)),
        ],
        compiler_params=pltpu.CompilerParams(
            collective_id=0, has_side_effects=True, vmem_limit_bytes=48 * 1024 * 1024
        ),
    )(
        normals, states, loadings, strikes.reshape(8, 256), hedge.reshape(8, 256),
        sigma.reshape(1, factors), tail,
    )


def solution(mesh):
    in_specs = (P("outer", "inner", None), P("outer", None), P(), P(), P(), P(), P())
    out_specs = P(("outer", "inner"), None)
    return jax.shard_map(body, mesh=mesh, in_specs=in_specs, out_specs=out_specs, check_vma=False)
```

time: 149 us -> 56.7 us (0.38); the launches traced: 147 us -> 56.4 us
  blocking collectives: 52 us -> 0 us
  Pallas kernels: 0 us -> 49 us
  waiting for transfers between devices: 31.4 us -> 0 us
  starting transfers between devices: 21.8 us -> 0 us
  matrix products: 15.7 us -> 0 us
  other arithmetic: 10.7 us -> 0 us
  local copies, waits for them, and re-layouts: 14.5 us -> 7.45 us
    all_to_all x1 -> x0, blocking collectives: 52 us -> none  [sum_at_owner(): lax.all_to_all(cut_along(value, dim, count), axis, 0, 0, tiled=True)]
    pallas_call x0 -> x1, Pallas kernels: none -> 49 us  [body(): pl.pallas_call(kernel, out_shape=jax.ShapeDtypeStruct((8, factors), F32),...]
    all_to_all x3 -> x0, waiting for transfers between devices: 31.4 us -> none  [the longest x1 15.3 us: sum_by_axis(): return jnp.sum(lax.all_to_all(own, far, 0, 0, tiled=True), axis=0)]
    all_to_all x3 -> x0, starting transfers between devices: 21.8 us -> none  [the longest x1 9.43 us: sum_by_axis(): return jnp.sum(lax.all_to_all(own, far, 0, 0, tiled=True), axis=0)]
    dot_general x2 -> x0, matrix products: 15.7 us -> none  [block(): lax.dot_general(weight, scaled_part.reshape(width * per_node, factors_n),...]
    gather x4 -> x0, local copies, waits for them, and re-layouts: 5.01 us -> none  [the longest x1 1.64 us: body(): local = jnp.clip(tail[safe] - group * node_count, 0, node_count - 1)]
    reduce_sum x4 -> x0, other arithmetic: 4.77 us -> none  [the longest x2 3.68 us: sum_at_owner(): return jnp.sum(blocks, axis=0)]
    transpose x1 -> x0, local copies, waits for them, and re-layouts: 2.81 us -> none  [cut_along(): return jnp.moveaxis(blocks, dim, 0)]
  transfers between devices with their start and end apart: 3 -> 0, of which waited for: 3 -> 0; matrix products, arithmetic and copies ran while one was open for 2% -> 0% of each run, Pallas kernels for 0% -> 0%
where the time goes in v1:
time: 56.7 us; the launch traced here: 56.4 us
  Pallas kernels  49 us (86%)
  local copies, waits for them, and re-layouts  7.45 us (13%)
    pallas_call x1, Pallas kernels, body(): pl.pallas_call(kernel, out_shape=jax.ShapeDtypeStruct((8, factors), F32),...  49 us
    unnamed x11, local copies, waits for them, and re-layouts  6.05 us

profile of v1, /device:TPU:1, one launch (start us, length us, event | category | flops | bytes accessed | tf_op | source)
XLA Modules:
  0.0 56.4 jit_solution(2832293637967710301)
XLA Ops:
  0.0 0.7 %reshape.9.strikes = f32[8,256]{1,0:T(8,128)S(1)} reshape(f32[2048]{0:T(1024)} %param.10) | data formatting | bytes 16384 | tf_op jit(solution)/shard_map/reshape | solution.py:416
  0.7 0.7 %reshape.10.hedge = f32[8,256]{1,0:T(8,128)S(1)} reshape(f32[2048]{0:T(1024)} %param.11) | data formatting | bytes 16384 | tf_op jit(solution)/shard_map/reshape | solution.py:416
  1.4 0.0 copy-start
  1.4 1.6 %copy-done = bf16[128,16,512]{2,1,0:T(8,128)(2,1)S(1)} copy-done((bf16[128,16,512]{2,1,0:T(8,128)(2,1)S(1)}, bf16[128,16,512]{2,1,0:T(8,128)(2,1)}, u32[]{:S(2)}) %copy-start) | copy-done | bytes 2097176
  3.0 0.0 copy-start.1
  3.0 1.6 %copy-done.1 = bf16[2048,512]{1,0:T(8,128)(2,1)S(1)} copy-done((bf16[2048,512]{1,0:T(8,128)(2,1)S(1)}, bf16[2048,512]{1,0:T(8,128)(2,1)}, u32[]{:S(2)}) %copy-start.1) | copy-done | bytes 2097176
  4.6 0.0 copy-start.2
  4.6 0.9 %copy-done.2 = bf16[128,512]{1,0:T(8,128)(2,1)S(1)} copy-done((bf16[128,512]{1,0:T(8,128)(2,1)S(1)}, bf16[128,512]{1,0:T(8,128)(2,1)}, u32[]{:S(2)}) %copy-start.2) | copy-done | bytes 131096
  5.5 0.0 copy-start.3
  5.5 0.7 %copy-done.3 = f32[512]{0:T(512)S(1)} copy-done((f32[512]{0:T(512)S(1)}, f32[512]{0:T(512)}, u32[]{:S(2)}) %copy-start.3) | copy-done | bytes 2072
  6.2 0.0 copy-start.4
  6.2 0.7 %copy-done.4 = s32[256]{0:T(256)S(1)} copy-done((s32[256]{0:T(256)S(1)}, s32[256]{0:T(256)}, u32[]{:S(2)}) %copy-start.4) | copy-done | bytes 1048
  6.8 49.0 %shard_map.73 = f32[8,512]{1,0:T(8,128)S(1)} custom-call(bf16[128,16,512]{2,1,0:T(8,128)(2,1)S(1)} %copy-done, bf16[128,512]{1,0:T(8,128)(2,1)S(1)} %copy-done.2, bf16[2048,512]{1,0:T(8,128)(2,1)S(1)} %copy-done.1, f32[8,256]{1,0:T(8,128)S(1)} %reshape.9.strikes, f32[8,256]{1,0:T(8,128)S(1)} %reshape.10.hedge, f32[1,512]{1,0:T(1,128)S(1)} %bitcast.1, ...), custom_call_target="tpu_custom_call" | custom-call | tf_op jit(solution)/shard_map/pallas_call | solution.py:356
  55.8 0.6 %copy.9 = f32[8,512]{1,0:T(8,128)} copy(f32[8,512]{1,0:T(8,128)S(1)} %shard_map.73) | data formatting | bytes 32768
Async XLA Ops:
  1.4 1.6 %copy-start = (bf16[128,16,512]{2,1,0:T(8,128)(2,1)S(1)}, bf16[128,16,512]{2,1,0:T(8,128)(2,1)}, u32[]{:S(2)}) copy-start(bf16[128,16,512]{2,1,0:T(8,128)(2,1)} %normals.1) | copy-start | bytes 6291460
  3.0 1.6 %copy-start.1 = (bf16[2048,512]{1,0:T(8,128)(2,1)S(1)}, bf16[2048,512]{1,0:T(8,128)(2,1)}, u32[]{:S(2)}) copy-start(bf16[2048,512]{1,0:T(8,128)(2,1)} %loadings.1) | copy-start | bytes 6291460
  4.6 0.9 %copy-start.2 = (bf16[128,512]{1,0:T(8,128)(2,1)S(1)}, bf16[128,512]{1,0:T(8,128)(2,1)}, u32[]{:S(2)}) copy-start(bf16[128,512]{1,0:T(8,128)(2,1)} %states.1) | copy-start | bytes 393220
  5.5 0.7 %copy-start.3 = (f32[512]{0:T(512)S(1)}, f32[512]{0:T(512)}, u32[]{:S(2)}) copy-start(f32[512]{0:T(512)} %param.12) | copy-start | bytes 6148
  6.2 0.7 %copy-start.4 = (s32[256]{0:T(256)S(1)}, s32[256]{0:T(256)}, u32[]{:S(2)}) copy-start(s32[256]{0:T(256)} %tail.1) | copy-start | bytes 3076

commit v2 on v1

v2 whole, which is shorter than its diff:
```python
import jax
import jax.numpy as jnp
from jax import lax
from jax.experimental import pallas as pl
from jax.experimental.pallas import tpu as pltpu
from jax.sharding import PartitionSpec as P

CAP = 80
EPSILON = 1e-06
CHUNKS = 4
BLOCKS = 5
MESH = pl.DeviceIdType.MESH
F32 = jnp.float32
BF16 = jnp.bfloat16


def place(hit):
    return jnp.where(hit, 1.0, 0.0)


def offsets():
    span = (0, 1, 2, 1)
    every = [(dx, dy, dc) for dx in range(4) for dy in range(4) for dc in range(2)][1:]
    return sorted(every, key=lambda d: -(span[d[0]] + span[d[1]]))


def code(dx, dy, dc):
    return (dx * 4 + dy) * 2 + dc


def kernel(
    normals, states, loadings, strikes, hedge, sigma, tail, out,
    held, own, pair, load_v, states_b, states_f, strikes_v, hedge_v, sigma_v, tail_s, slot_s, live_s,
    sums, sums_in, stats, half_strike, half_hedge, own_load, load_t,
    mixed, part, turned, weight, sent, in_x, in_y, mid_x, mid_y, in_xy, in_yx, last, in_z,
    copy_sem, pair_sem, sum_out, sum_in, stat_out, stat_in,
    x_out, x_in, y_out, y_in, xy_out, xy_in, yx_out, yx_in, z_out, z_in,
):
    z = lax.axis_index("outer")
    me = lax.axis_index("inner")
    x, y, c = lax.div(me, 8), lax.rem(lax.div(me, 2), 4), lax.rem(me, 2)
    nodes, per_node, factors = held.shape
    paths = per_node * 32
    tails = tail_s.shape[0]
    others = offsets()

    def device(dx, dy, dc):
        return (lax.rem(x + dx, 4) * 4 + lax.rem(y + dy, 4)) * 2 + lax.rem(c + dc, 2)

    copies = [
        (tail, tail_s), (normals, held), (states, states_b), (sigma, sigma_v), (loadings, load_v),
    ]
    for i in range(8):
        copies.append((strikes.at[pl.ds(i * 256, 256)], strikes_v.at[i]))
        copies.append((hedge.at[pl.ds(i * 256, 256)], hedge_v.at[i]))
    loads = [pltpu.make_async_copy(a, b, copy_sem.at[i]) for i, (a, b) in enumerate(copies)]
    loads[0].start()
    loads[1].start()

    barrier = pltpu.get_barrier_semaphore()

    def greet(where):
        pl.semaphore_signal(barrier, inc=1, device_id=where, device_id_type=MESH)

    for d in others:
        greet((z, device(*d)))
    for d in (4, 3, 5, 2, 6, 1, 7):
        greet((lax.rem(z + d, 8), me))
    for item in loads[2:]:
        item.start()

    loads[0].wait()
    first = jnp.int32(0)
    step = tails // 2
    while step:
        first = first + jnp.where(tail_s[first + step - 1] < z * nodes, step, 0)
        step //= 2

    def find(s, carry):
        at = jnp.minimum(first + s, tails - 1)
        node = tail_s[at] - z * nodes
        good = (first + s < tails) & (node >= 0) & (node < nodes)
        slot_s[s] = jnp.clip(node, 0, nodes - 1)
        live_s[s] = jnp.where(good, 1.0, 0.0).astype(F32)
        return carry

    lax.fori_loop(0, CAP, find, 0, unroll=8)
    loads[1].wait()

    def add_up(q, carry):
        for i in range(5):
            rows = held[slot_s[q * 5 + i]]
            own[q * 5 + i] = rows
            block = rows.astype(F32)
            one = jnp.sum(block, axis=0, keepdims=True)
            two = jnp.sum(block * block, axis=0, keepdims=True)
            for h in range(2):
                for b in range(2):
                    lanes = slice(h * 256 + b * 128, h * 256 + b * 128 + 128)
                    sums[q * 2 + h, i, b : b + 1, :] = one[:, lanes]
                    sums[q * 2 + h, i, 2 + b : 3 + b, :] = two[:, lanes]
        return carry

    lax.fori_loop(0, 16, add_up, 0)
    pl.semaphore_wait(barrier, 38)

    def sum_copy(d):
        k = code(*d)
        return pltpu.make_async_remote_copy(
            src_ref=sums.at[device(*d)], dst_ref=sums_in.at[k],
            send_sem=sum_out.at[k], recv_sem=sum_in.at[k],
            device_id=(z, device(*d)), device_id_type=MESH,
        )

    def stat_copy(d):
        k = code(*d)
        return pltpu.make_async_remote_copy(
            src_ref=stats.at[0], dst_ref=stats.at[k],
            send_sem=stat_out.at[k], recv_sem=stat_in.at[k],
            device_id=(z, device(*d)), device_id_type=MESH,
        )

    for d in others:
        sum_copy(d).start()
    swap = pltpu.make_async_remote_copy(
        src_ref=own, dst_ref=pair, send_sem=pair_sem.at[0], recv_sem=pair_sem.at[1],
        device_id=(z, device(0, 0, 1)), device_id_type=MESH,
    )
    swap.start()

    for item in loads[2:]:
        item.wait()
    states_f[...] = states_b[...].astype(F32)
    m_id = lax.broadcasted_iota(jnp.int32, (256, 256), 0)
    l_id = lax.broadcasted_iota(jnp.int32, (256, 256), 1)
    same = (m_id // 16 == l_id // 16) & (m_id % 8 == l_id % 8)
    picks = [same & ((m_id // 8) % 2 == c) & ((l_id // 8) % 2 == a) for a in range(2)]
    picks_t = [same & ((l_id // 8) % 2 == c) & ((m_id // 8) % 2 == a) for a in range(2)]
    for source, target in ((strikes_v, half_strike), (hedge_v, half_hedge)):
        rows = source[...] * 0.5
        moved = [
            jnp.dot(rows, place(pick), precision=lax.Precision.HIGHEST, preferred_element_type=F32)
            for pick in picks
        ]
        for j in range(CHUNKS):
            target[j] = moved[0][2 * j : 2 * j + 1] + moved[1][2 * j + 1 : 2 * j + 2]
    turn = [place(pick).astype(BF16) for pick in picks_t]

    def order(j, carry):
        rows = jnp.zeros((256, factors), F32)
        for a in range(2):
            at = pl.multiple_of((2 * j + a) * 256, 256)
            rows = rows + jnp.dot(turn[a], load_v[pl.ds(at, 256), :], preferred_element_type=F32)
        own_load[j] = rows
        load_t[j] = (rows * 0.5).astype(BF16).T
        return carry

    lax.fori_loop(0, CHUNKS, order, 0)

    total = sums[me]
    for d in reversed(others):
        sum_copy(d).wait_recv()
        total = total + sums_in[code(*d)]
    center = total[:, 0:2, :] / paths
    spread = total[:, 2:4, :] / paths - center * center
    stats[0, :, 0:2, :] = center
    stats[0, :, 2:4, :] = lax.rsqrt(spread + EPSILON)
    for d in others:
        stat_copy(d).start()
    for d in others:
        sum_copy(d).wait_send()
    swap.wait()

    def normalise(g):
        dx = (0, 1, 3, 2)[g]
        for u in range(4):
            dy = (0, 1, 3, 2)[u]
            for dc in range(2):
                if dx or dy or dc:
                    stat_copy((dx, dy, dc)).wait_recv()
        for u in range(4):
            dy = (0, 1, 3, 2)[u]
            q = lax.rem(x + 4 - dx, 4) * 4 + lax.rem(y + 4 - dy, 4)
            for i in range(5):
                s = q * 5 + i
                at, live = slot_s[s], live_s[s]
                state = states_f[pl.ds(at, 1), :]
                for e, source in enumerate((own, pair)):
                    block = source[s]
                    row = (g * 4 + u) * 160 + i * 32 + e * 16
                    for lane in range(4):
                        h, b = lane // 2, lane % 2
                        lanes = slice(lane * 128, lane * 128 + 128)
                        k = code(dx, dy, 0) + lax.rem(c + h, 2)
                        mean = stats[k, i, b : b + 1, :]
                        scale = stats[k, i, 2 + b : 3 + b, :] * live
                        scaled = ((block[:, lanes].astype(F32) - mean) * scale).astype(BF16)
                        both = state[:, lanes] + sigma_v[:, lanes] * scaled.astype(F32)
                        mixed[row : row + 16, lanes] = both.astype(BF16)
                        part[row : row + 16, lanes] = scaled

    def turn_over(g):
        for b in range(5):
            at = g * 640 + b * 128
            turned[:, at : at + 128] = part[at : at + 128, :].T

    def weigh(j, at, count):
        level = jnp.dot(mixed[at : at + count, :], load_t[j], preferred_element_type=F32)
        size = half_hedge[j]
        fresh = size + size * jnp.tanh(level - half_strike[j])
        weight[j % 2, at : at + count, :] = fresh.astype(BF16)

    def x_copy(j, r):
        px = lax.rem(x + r, 4)
        return pltpu.make_async_remote_copy(
            src_ref=sent.at[j, px, :, :, pl.ds(0, 256)], dst_ref=in_x.at[j, r - 1],
            send_sem=x_out.at[j, r - 1], recv_sem=x_in.at[j, r - 1],
            device_id=(z, device(r, 0, 0)), device_id_type=MESH,
        )

    def y_copy(j, r):
        py = lax.rem(y + r, 4)
        return pltpu.make_async_remote_copy(
            src_ref=sent.at[j, :, py, :, pl.ds(256, 256)], dst_ref=in_y.at[j, r - 1],
            send_sem=y_out.at[j, r - 1], recv_sem=y_in.at[j, r - 1],
            device_id=(z, device(0, r, 0)), device_id_type=MESH,
        )

    def xy_copy(j, r):
        py = lax.rem(y + r, 4)
        return pltpu.make_async_remote_copy(
            src_ref=mid_x.at[j, py], dst_ref=in_xy.at[j, r - 1],
            send_sem=xy_out.at[j, r - 1], recv_sem=xy_in.at[j, r - 1],
            device_id=(z, device(0, r, 0)), device_id_type=MESH,
        )

    def yx_copy(j, r):
        px = lax.rem(x + r, 4)
        return pltpu.make_async_remote_copy(
            src_ref=mid_y.at[j, px], dst_ref=in_yx.at[j, r - 1],
            send_sem=yx_out.at[j, r - 1], recv_sem=yx_in.at[j, r - 1],
            device_id=(z, device(r, 0, 0)), device_id_type=MESH,
        )

    def z_copy(j, a, slot):
        return pltpu.make_async_remote_copy(
            src_ref=last.at[j, a], dst_ref=in_z.at[slot],
            send_sem=z_out.at[j, a], recv_sem=z_in.at[slot],
            device_id=(2 * j + a, me), device_id_type=MESH,
        )

    def finish(j):
        rows = jnp.dot(turned[...], weight[j % 2], preferred_element_type=F32)
        sent[j] = rows.astype(BF16).T.reshape(4, 4, 16, factors)
        for r in (2, 1, 3):
            x_copy(j, r).start()
            y_copy(j, r).start()

    def second(j):
        for r in (1, 3, 2):
            x_copy(j, r).wait_recv()
        total = sent[j, x, :, :, 0:256].astype(F32)
        for r in range(3):
            total = total + in_x[j, r].astype(F32)
        mid_x[j] = total
        for r in (1, 3, 2):
            y_copy(j, r).wait_recv()
        for r in (2, 1, 3):
            xy_copy(j, r).start()
        total = sent[j, :, y, :, 256:512].astype(F32)
        for r in range(3):
            total = total + in_y[j, r].astype(F32)
        mid_y[j] = total
        for r in (2, 1, 3):
            yx_copy(j, r).start()

    def third(j):
        for r in (1, 3, 2):
            xy_copy(j, r).wait_recv()
        one = mid_x[j, y]
        for r in range(3):
            one = one + in_xy[j, r]
        for r in (1, 3, 2):
            yx_copy(j, r).wait_recv()
        two = mid_y[j, x]
        for r in range(3):
            two = two + in_yx[j, r]
        for a in range(2):
            last[j, a, :, 0:256] = one[a * 8 : a * 8 + 8]
            last[j, a, :, 256:512] = two[a * 8 : a * 8 + 8]
        for a in range(2):
            @pl.when(z != 2 * j + a)
            def _():
                z_copy(j, a, lax.rem(z - (2 * j + a) + 8, 8) - 1).start()

    for g in range(4):
        normalise(g)
        if g:
            turn_over(g - 1)
            weigh(0, (g - 1) * 640, 640)
    turn_over(3)
    weigh(0, 1920, 640)
    for j in range(1, CHUNKS + 1):
        if j < CHUNKS:
            for b in range(BLOCKS):
                weigh(j, b * 512, 512)
        finish(j - 1)
    for d in others:
        stat_copy(d).wait_send()
    for j in range(CHUNKS):
        second(j)
    for j in range(CHUNKS):
        for r in (1, 2, 3):
            x_copy(j, r).wait_send()
            y_copy(j, r).wait_send()
    for j in range(CHUNKS):
        third(j)

    for j in range(CHUNKS):
        for r in (1, 2, 3):
            xy_copy(j, r).wait_send()
            yx_copy(j, r).wait_send()
    for slot in range(7):
        z_copy(0, 0, slot).wait_recv()
    total = last[lax.div(z, 2), lax.rem(z, 2)]
    for slot in range(7):
        total = total + in_z[slot]
    at = pl.multiple_of((x * 4 + y) * 16 + lax.rem(z, 2) * 8, 8)
    out[...] = own_load[lax.div(z, 2), pl.ds(at, 8), :] * total / (tails * paths)

    for j in range(CHUNKS):
        for a in range(2):
            @pl.when(z != 2 * j + a)
            def _():
                z_copy(j, a, 0).wait_send()


def body(normals, states, loadings, strikes, hedge, sigma, tail):
    nodes, per_node, factors = normals.shape
    rows = CAP * per_node * 2
    dma = pltpu.SemaphoreType.DMA
    return pl.pallas_call(
        kernel,
        out_shape=jax.ShapeDtypeStruct((8, factors), F32),
        in_specs=[pl.BlockSpec(memory_space=pltpu.HBM)] * 7,
        out_specs=pl.BlockSpec(memory_space=pltpu.VMEM),
        scratch_shapes=[
            pltpu.VMEM(normals.shape, BF16),
            pltpu.VMEM((CAP, per_node, factors), BF16),
            pltpu.VMEM((CAP, per_node, factors), BF16),
            pltpu.VMEM(loadings.shape, BF16),
            pltpu.VMEM(states.shape, BF16),
            pltpu.VMEM(states.shape, F32),
            pltpu.VMEM((8, 256), F32),
            pltpu.VMEM((8, 256), F32),
            pltpu.VMEM((1, factors), F32),
            pltpu.SMEM(tail.shape, jnp.int32),
            pltpu.SMEM((CAP,), jnp.int32),
            pltpu.SMEM((CAP,), F32),
            pltpu.VMEM((32, 5, 4, 128), F32),
            pltpu.VMEM((32, 5, 4, 128), F32),
            pltpu.VMEM((32, 5, 4, 128), F32),
            pltpu.VMEM((CHUNKS, 1, 256), F32),
            pltpu.VMEM((CHUNKS, 1, 256), F32),
            pltpu.VMEM((CHUNKS, 256, factors), F32),
            pltpu.VMEM((CHUNKS, factors, 256), BF16),
            pltpu.VMEM((rows, factors), BF16),
            pltpu.VMEM((rows, factors), BF16),
            pltpu.VMEM((factors, rows), BF16),
            pltpu.VMEM((2, rows, 256), BF16),
            pltpu.VMEM((CHUNKS, 4, 4, 16, factors), BF16),
            pltpu.VMEM((CHUNKS, 3, 4, 16, 256), BF16),
            pltpu.VMEM((CHUNKS, 3, 4, 16, 256), BF16),
            pltpu.VMEM((CHUNKS, 4, 16, 256), F32),
            pltpu.VMEM((CHUNKS, 4, 16, 256), F32),
            pltpu.VMEM((CHUNKS, 3, 16, 256), F32),
            pltpu.VMEM((CHUNKS, 3, 16, 256), F32),
            pltpu.VMEM((CHUNKS, 2, 8, factors), F32),
            pltpu.VMEM((7, 8, factors), F32),
            dma((21,)),
            dma((2,)),
            dma((32,)),
            dma((32,)),
            dma((32,)),
            dma((32,)),
            dma((CHUNKS, 3)),
            dma((CHUNKS, 3)),
            dma((CHUNKS, 3)),
            dma((CHUNKS, 3)),
            dma((CHUNKS, 3)),
            dma((CHUNKS, 3)),
            dma((CHUNKS, 3)),
            dma((CHUNKS, 3)),
            dma((CHUNKS, 2)),
            dma((7,)),
        ],
        compiler_params=pltpu.CompilerParams(
            collective_id=0, has_side_effects=True, vmem_limit_bytes=63 * 1024 * 1024
        ),
    )(
        normals, states, loadings, strikes, hedge, sigma.reshape(1, factors), tail,
    )


def solution(mesh):
    in_specs = (P("outer", "inner", None), P("outer", None), P(), P(), P(), P(), P())
    out_specs = P(("outer", "inner"), None)
    return jax.shard_map(body, mesh=mesh, in_specs=in_specs, out_specs=out_specs, check_vma=False)
```

time: 56.7 us -> 44.9 us (0.79)
  local copies, waits for them, and re-layouts: 7.45 us -> 1.32 us
  Pallas kernels: 49 us -> 43.4 us
    pallas_call x1, Pallas kernels: 49 us -> 43.4 us  [body(): pl.pallas_call(kernel, out_shape=jax.ShapeDtypeStruct((8, factors), F32),...]
    unnamed x11 -> x1, local copies, waits for them, and re-layouts: 6.05 us -> 1.32 us
    reshape x2 -> x0, local copies, waits for them, and re-layouts: 1.4 us -> none  [the longest x1 0.7 us: body(): strikes.reshape(8, 256)]
where the time goes in v2:
time: 44.9 us; the launch traced here: 44.7 us
  Pallas kernels  43.4 us (97%)
  local copies, waits for them, and re-layouts  1.32 us (3%)
    pallas_call x1, Pallas kernels, body(): pl.pallas_call(kernel, out_shape=jax.ShapeDtypeStruct((8, factors), F32),...  43.4 us
    unnamed x1, local copies, waits for them, and re-layouts  1.32 us

profile of v2, /device:TPU:1, one launch (start us, length us, event | category | flops | bytes accessed | tf_op | source)
XLA Modules:
  0.0 44.7 jit_solution(2107372910129060945)
XLA Ops:
  0.0 43.4 %shard_map.73 = f32[8,512]{1,0:T(8,128)} custom-call(bf16[128,16,512]{2,1,0:T(8,128)(2,1)} %normals.1, bf16[128,512]{1,0:T(8,128)(2,1)} %states.1, bf16[2048,512]{1,0:T(8,128)(2,1)} %loadings.1, f32[2048]{0:T(1024)} %strikes.1, f32[2048]{0:T(1024)} %hedge.1, f32[1,512]{1,0:T(1,128)} %bitcast.1, s32[256]{0:T(256)} %tail.1), custom_call_target="tpu_custom_call" | custom-call | tf_op jit(solution)/shard_map/pallas_call | solution.py:342
  43.4 1.3 %copy.9 = f32[8,512]{1,0:T(8,128)} copy(f32[8,512]{1,0:T(8,128)} %shard_map.73) | data formatting | bytes 32768

commit v3 on v2

--- a/solution.py
+++ b/solution.py
@@ -20,20 +20,16 @@
 
 def offsets():
     span = (0, 1, 2, 1)
-    every = [(dx, dy, dc) for dx in range(4) for dy in range(4) for dc in range(2)][1:]
+    every = [(dx, dy) for dx in range(4) for dy in range(4)][1:]
     return sorted(every, key=lambda d: -(span[d[0]] + span[d[1]]))
-
-
-def code(dx, dy, dc):
-    return (dx * 4 + dy) * 2 + dc
 
 
 def kernel(
     normals, states, loadings, strikes, hedge, sigma, tail, out,
-    held, own, pair, load_v, states_b, states_f, strikes_v, hedge_v, sigma_v, tail_s, slot_s, live_s,
-    sums, sums_in, stats, half_strike, half_hedge, own_load, load_t,
+    held, own, pair, load_v, states_b, states_f, strikes_v, hedge_v, sigma_v, sigma_f, tail_s, slot_s, live_s,
+    sums, sums_pair, sums_chip, sums_in, stats, half_strike, half_hedge, own_load, load_t,
     mixed, part, turned, weight, sent, in_x, in_y, mid_x, mid_y, in_xy, in_yx, last, in_z,
-    copy_sem, pair_sem, sum_out, sum_in, stat_out, stat_in,
+    copy_sem, pair_sem, join_sem, pass_sem, sum_out, sum_in, stat_out, stat_in,
     x_out, x_in, y_out, y_in, xy_out, xy_in, yx_out, yx_in, z_out, z_in,
 ):
     z = lax.axis_index("outer")
@@ -62,10 +58,12 @@
     def greet(where):
         pl.semaphore_signal(barrier, inc=1, device_id=where, device_id_type=MESH)
 
-    for d in others:
-        greet((z, device(*d)))
+    for dx, dy in others:
+        greet((z, device(dx, dy, 0)))
     for d in (4, 3, 5, 2, 6, 1, 7):
         greet((lax.rem(z + d, 8), me))
+    partner = (z, device(0, 0, 1))
+    greet(partner)
     for item in loads[2:]:
         item.start()
 
@@ -97,40 +95,52 @@
             for h in range(2):
                 for b in range(2):
                     lanes = slice(h * 256 + b * 128, h * 256 + b * 128 + 128)
-                    sums[q * 2 + h, i, b : b + 1, :] = one[:, lanes]
-                    sums[q * 2 + h, i, 2 + b : 3 + b, :] = two[:, lanes]
+                    sums[h, q, i, b : b + 1, :] = one[:, lanes]
+                    sums[h, q, i, 2 + b : 3 + b, :] = two[:, lanes]
         return carry
 
     lax.fori_loop(0, 16, add_up, 0)
-    pl.semaphore_wait(barrier, 38)
+    pl.semaphore_wait(barrier, 23)
+
+    join = pltpu.make_async_remote_copy(
+        src_ref=sums.at[1 - c], dst_ref=sums_pair, send_sem=join_sem.at[0], recv_sem=join_sem.at[1],
+        device_id=partner, device_id_type=MESH,
+    )
+    join.start()
+    for item in loads[2:]:
+        item.wait()
+    for b in range(4):
+        lanes = slice(b * 128, b * 128 + 128)
+        states_f[b] = states_b[:, lanes].astype(F32)
+        sigma_f[b] = sigma_v[:, lanes]
+    join.wait_recv()
+    sums_chip[...] = sums[c] + sums_pair[...]
 
     def sum_copy(d):
-        k = code(*d)
-        return pltpu.make_async_remote_copy(
-            src_ref=sums.at[device(*d)], dst_ref=sums_in.at[k],
-            send_sem=sum_out.at[k], recv_sem=sum_in.at[k],
-            device_id=(z, device(*d)), device_id_type=MESH,
+        dx, dy = d
+        return pltpu.make_async_remote_copy(
+            src_ref=sums_chip.at[lax.rem(x + dx, 4) * 4 + lax.rem(y + dy, 4)],
+            dst_ref=sums_in.at[dx * 4 + dy],
+            send_sem=sum_out.at[dx * 4 + dy], recv_sem=sum_in.at[dx * 4 + dy],
+            device_id=(z, device(dx, dy, 0)), device_id_type=MESH,
         )
 
     def stat_copy(d):
-        k = code(*d)
-        return pltpu.make_async_remote_copy(
-            src_ref=stats.at[0], dst_ref=stats.at[k],
-            send_sem=stat_out.at[k], recv_sem=stat_in.at[k],
-            device_id=(z, device(*d)), device_id_type=MESH,
+        dx, dy = d
+        return pltpu.make_async_remote_copy(
+            src_ref=stats.at[0, 0], dst_ref=stats.at[0, dx * 4 + dy],
+            send_sem=stat_out.at[dx * 4 + dy], recv_sem=stat_in.at[dx * 4 + dy],
+            device_id=(z, device(dx, dy, 0)), device_id_type=MESH,
         )
 
     for d in others:
         sum_copy(d).start()
     swap = pltpu.make_async_remote_copy(
         src_ref=own, dst_ref=pair, send_sem=pair_sem.at[0], recv_sem=pair_sem.at[1],
-        device_id=(z, device(0, 0, 1)), device_id_type=MESH,
+        device_id=partner, device_id_type=MESH,
     )
     swap.start()
 
-    for item in loads[2:]:
-        item.wait()
-    states_f[...] = states_b[...].astype(F32)
     m_id = lax.broadcasted_iota(jnp.int32, (256, 256), 0)
     l_id = lax.broadcasted_iota(jnp.int32, (256, 256), 1)
     same = (m_id // 16 == l_id // 16) & (m_id % 8 == l_id % 8)
@@ -157,45 +167,45 @@
 
     lax.fori_loop(0, CHUNKS, order, 0)
 
-    total = sums[me]
+    total = sums_chip[x * 4 + y]
     for d in reversed(others):
         sum_copy(d).wait_recv()
-        total = total + sums_in[code(*d)]
+        total = total + sums_in[d[0] * 4 + d[1]]
     center = total[:, 0:2, :] / paths
     spread = total[:, 2:4, :] / paths - center * center
-    stats[0, :, 0:2, :] = center
-    stats[0, :, 2:4, :] = lax.rsqrt(spread + EPSILON)
+    stats[0, 0, :, 0:2, :] = center
+    stats[0, 0, :, 2:4, :] = lax.rsqrt(spread + EPSILON)
     for d in others:
         stat_copy(d).start()
     for d in others:
         sum_copy(d).wait_send()
+    join.wait_send()
     swap.wait()
-
-    def normalise(g):
-        dx = (0, 1, 3, 2)[g]
-        for u in range(4):
-            dy = (0, 1, 3, 2)[u]
-            for dc in range(2):
-                if dx or dy or dc:
-                    stat_copy((dx, dy, dc)).wait_recv()
-        for u in range(4):
-            dy = (0, 1, 3, 2)[u]
-            q = lax.rem(x + 4 - dx, 4) * 4 + lax.rem(y + 4 - dy, 4)
+    for d in reversed(others):
+        stat_copy(d).wait_recv()
+    give = pltpu.make_async_remote_copy(
+        src_ref=stats.at[0], dst_ref=stats.at[1], send_sem=pass_sem.at[0], recv_sem=pass_sem.at[1],
+        device_id=partner, device_id_type=MESH,
+    )
+    give.start()
+
+    def normalise(g, e):
+        base = (c if e == 0 else 1 - c) * 2
+        for dy in range(4):
+            q = lax.rem(x + 4 - g, 4) * 4 + lax.rem(y + 4 - dy, 4)
             for i in range(5):
                 s = q * 5 + i
                 at, live = slot_s[s], live_s[s]
-                state = states_f[pl.ds(at, 1), :]
-                for e, source in enumerate((own, pair)):
-                    block = source[s]
-                    row = (g * 4 + u) * 160 + i * 32 + e * 16
-                    for lane in range(4):
-                        h, b = lane // 2, lane % 2
-                        lanes = slice(lane * 128, lane * 128 + 128)
-                        k = code(dx, dy, 0) + lax.rem(c + h, 2)
-                        mean = stats[k, i, b : b + 1, :]
-                        scale = stats[k, i, 2 + b : 3 + b, :] * live
-                        scaled = ((block[:, lanes].astype(F32) - mean) * scale).astype(BF16)
-                        both = state[:, lanes] + sigma_v[:, lanes] * scaled.astype(F32)
+                for b in range(2):
+                    lanes = pl.ds(pl.multiple_of((base + b) * 128, 128), 128)
+                    state = states_f[base + b, pl.ds(at, 1), :]
+                    mean = stats[e, g * 4 + dy, i, b : b + 1, :]
+                    scale = stats[e, g * 4 + dy, i, 2 + b : 3 + b, :] * live
+                    for w, source in enumerate((own, pair)):
+                        row = (g * 4 + dy) * 160 + i * 32 + w * 16
+                        block = source[s, :, lanes].astype(F32)
+                        scaled = ((block - mean) * scale).astype(BF16)
+                        both = state + sigma_f[base + b] * scaled.astype(F32)
                         mixed[row : row + 16, lanes] = both.astype(BF16)
                         part[row : row + 16, lanes] = scaled
 
@@ -294,7 +304,10 @@
                 z_copy(j, a, lax.rem(z - (2 * j + a) + 8, 8) - 1).start()
 
     for g in range(4):
-        normalise(g)
+        normalise(g, 0)
+    give.wait_recv()
+    for g in range(4):
+        normalise(g, 1)
         if g:
             turn_over(g - 1)
             weigh(0, (g - 1) * 640, 640)
@@ -305,16 +318,21 @@
             for b in range(BLOCKS):
                 weigh(j, b * 512, 512)
         finish(j - 1)
+    give.wait_send()
     for d in others:
         stat_copy(d).wait_send()
-    for j in range(CHUNKS):
-        second(j)
+    second(0)
+    second(1)
+    second(2)
+    third(0)
     for j in range(CHUNKS):
         for r in (1, 2, 3):
             x_copy(j, r).wait_send()
             y_copy(j, r).wait_send()
-    for j in range(CHUNKS):
-        third(j)
+    second(3)
+    third(1)
+    third(2)
+    third(3)
 
     for j in range(CHUNKS):
         for r in (1, 2, 3):
@@ -350,16 +368,19 @@
             pltpu.VMEM((CAP, per_node, factors), BF16),
             pltpu.VMEM(loadings.shape, BF16),
             pltpu.VMEM(states.shape, BF16),
-            pltpu.VMEM(states.shape, F32),
+            pltpu.VMEM((4, nodes, 128), F32),
             pltpu.VMEM((8, 256), F32),
             pltpu.VMEM((8, 256), F32),
             pltpu.VMEM((1, factors), F32),
+            pltpu.VMEM((4, 1, 128), F32),
             pltpu.SMEM(tail.shape, jnp.int32),
             pltpu.SMEM((CAP,), jnp.int32),
             pltpu.SMEM((CAP,), F32),
-            pltpu.VMEM((32, 5, 4, 128), F32),
-            pltpu.VMEM((32, 5, 4, 128), F32),
-            pltpu.VMEM((32, 5, 4, 128), F32),
+            pltpu.VMEM((2, 16, 5, 4, 128), F32),
+            pltpu.VMEM((16, 5, 4, 128), F32),
+            pltpu.VMEM((16, 5, 4, 128), F32),
+            pltpu.VMEM((16, 5, 4, 128), F32),
+            pltpu.VMEM((2, 16, 5, 4, 128), F32),
             pltpu.VMEM((CHUNKS, 1, 256), F32),
             pltpu.VMEM((CHUNKS, 1, 256), F32),
             pltpu.VMEM((CHUNKS, 256, factors), F32),
@@ -379,10 +400,12 @@
             pltpu.VMEM((7, 8, factors), F32),
             dma((21,)),
             dma((2,)),
-            dma((32,)),
-            dma((32,)),
-            dma((32,)),
-            dma((32,)),
+            dma((2,)),
+            dma((2,)),
+            dma((16,)),
+            dma((16,)),
+            dma((16,)),
+            dma((16,)),
             dma((CHUNKS, 3)),
             dma((CHUNKS, 3)),
             dma((CHUNKS, 3)),

time: 44.9 us -> 44.2 us (0.984)
  Pallas kernels: 43.4 us -> 42.7 us
    pallas_call x1, Pallas kernels: 43.4 us -> 42.7 us  [body(): pl.pallas_call(kernel, out_shape=jax.ShapeDtypeStruct((8, factors), F32),...]
where the time goes in v3:
time: 44.2 us; the launch traced here: 44.1 us
  Pallas kernels  42.7 us (97%)
  local copies, waits for them, and re-layouts  1.32 us (3%)
    pallas_call x1, Pallas kernels, body(): pl.pallas_call(kernel, out_shape=jax.ShapeDtypeStruct((8, factors), F32),...  42.7 us
    unnamed x1, local copies, waits for them, and re-layouts  1.32 us

profile of v3, /device:TPU:1, one launch (start us, length us, event | category | flops | bytes accessed | tf_op | source)
XLA Modules:
  0.0 44.1 jit_solution(2630638441744522979)
XLA Ops:
  0.0 42.7 %shard_map.73 = f32[8,512]{1,0:T(8,128)} custom-call(bf16[128,16,512]{2,1,0:T(8,128)(2,1)} %normals.1, bf16[128,512]{1,0:T(8,128)(2,1)} %states.1, bf16[2048,512]{1,0:T(8,128)(2,1)} %loadings.1, f32[2048]{0:T(1024)} %strikes.1, f32[2048]{0:T(1024)} %hedge.1, f32[1,512]{1,0:T(1,128)} %bitcast.1, s32[256]{0:T(256)} %tail.1), custom_call_target="tpu_custom_call" | custom-call | tf_op jit(solution)/shard_map/pallas_call | solution.py:360
  42.7 1.3 %copy.9 = f32[8,512]{1,0:T(8,128)} copy(f32[8,512]{1,0:T(8,128)} %shard_map.73) | data formatting | bytes 32768

commit v4 on v3

--- a/solution.py
+++ b/solution.py
@@ -8,7 +8,6 @@
 CAP = 80
 EPSILON = 1e-06
 CHUNKS = 4
-BLOCKS = 5
 MESH = pl.DeviceIdType.MESH
 F32 = jnp.float32
 BF16 = jnp.bfloat16
@@ -259,9 +258,12 @@
             device_id=(2 * j + a, me), device_id_type=MESH,
         )
 
-    def finish(j):
-        rows = jnp.dot(turned[...], weight[j % 2], preferred_element_type=F32)
-        sent[j] = rows.astype(BF16).T.reshape(4, 4, 16, factors)
+    def cross(j, h):
+        at = h * 256
+        rows = jnp.dot(turned[at : at + 256, :], weight[j % 2], preferred_element_type=F32)
+        sent[j, :, :, :, at : at + 256] = rows.astype(BF16).T.reshape(4, 4, 16, 256)
+
+    def travel(j):
         for r in (2, 1, 3):
             x_copy(j, r).start()
             y_copy(j, r).start()
@@ -314,25 +316,25 @@
     turn_over(3)
     weigh(0, 1920, 640)
     for j in range(1, CHUNKS + 1):
-        if j < CHUNKS:
-            for b in range(BLOCKS):
-                weigh(j, b * 512, 512)
-        finish(j - 1)
+        for h in range(2):
+            if j < CHUNKS:
+                weigh(j, h * 1280, 640)
+                weigh(j, h * 1280 + 640, 640)
+            cross(j - 1, h)
+        if j == CHUNKS:
+            second(0)
+        travel(j - 1)
     give.wait_send()
     for d in others:
         stat_copy(d).wait_send()
-    second(0)
-    second(1)
-    second(2)
-    third(0)
+    for j in range(1, CHUNKS):
+        second(j)
     for j in range(CHUNKS):
         for r in (1, 2, 3):
             x_copy(j, r).wait_send()
             y_copy(j, r).wait_send()
-    second(3)
-    third(1)
-    third(2)
-    third(3)
+    for j in range(CHUNKS):
+        third(j)
 
     for j in range(CHUNKS):
         for r in (1, 2, 3):

time: 44.2 us -> 43.4 us (0.982)
  Pallas kernels: 42.7 us -> 41.9 us
    pallas_call x1, Pallas kernels: 42.7 us -> 41.9 us  [body(): pl.pallas_call(kernel, out_shape=jax.ShapeDtypeStruct((8, factors), F32),...]
where the time goes in v4:
time: 43.4 us; the launch traced here: 43.2 us
  Pallas kernels  41.9 us (97%)
  local copies, waits for them, and re-layouts  1.32 us (3%)
    pallas_call x1, Pallas kernels, body(): pl.pallas_call(kernel, out_shape=jax.ShapeDtypeStruct((8, factors), F32),...  41.9 us
    unnamed x1, local copies, waits for them, and re-layouts  1.32 us

profile of v4, /device:TPU:1, one launch (start us, length us, event | category | flops | bytes accessed | tf_op | source)
XLA Modules:
  0.0 43.2 jit_solution(9472451856557227254)
XLA Ops:
  0.0 41.9 %shard_map.73 = f32[8,512]{1,0:T(8,128)} custom-call(bf16[128,16,512]{2,1,0:T(8,128)(2,1)} %normals.1, bf16[128,512]{1,0:T(8,128)(2,1)} %states.1, bf16[2048,512]{1,0:T(8,128)(2,1)} %loadings.1, f32[2048]{0:T(1024)} %strikes.1, f32[2048]{0:T(1024)} %hedge.1, f32[1,512]{1,0:T(1,128)} %bitcast.1, s32[256]{0:T(256)} %tail.1), custom_call_target="tpu_custom_call" | custom-call | tf_op jit(solution)/shard_map/pallas_call | solution.py:362
  41.9 1.3 %copy.9 = f32[8,512]{1,0:T(8,128)} copy(f32[8,512]{1,0:T(8,128)} %shard_map.73) | data formatting | bytes 32768

commit v5 on v4

--- a/solution.py
+++ b/solution.py
@@ -361,7 +361,7 @@
     dma = pltpu.SemaphoreType.DMA
     return pl.pallas_call(
         kernel,
-        out_shape=jax.ShapeDtypeStruct((8, factors), F32),
+        out_shape=pltpu.VMEM((8, factors), F32),
         in_specs=[pl.BlockSpec(memory_space=pltpu.HBM)] * 7,
         out_specs=pl.BlockSpec(memory_space=pltpu.VMEM),
         scratch_shapes=[

time: 43.4 us -> 42 us (0.968)
  local copies, waits for them, and re-layouts: 1.32 us -> 0.61 us
  Pallas kernels: 41.9 us -> 41.3 us
    unnamed x1, local copies, waits for them, and re-layouts: 1.32 us -> 0.61 us
    pallas_call x1, Pallas kernels: 41.9 us -> 41.3 us  [body(): pl.pallas_call(kernel, out_shape=pltpu.VMEM((8, factors), F32), in_specs=...]
where the time goes in v5:
time: 42 us; the launch traced here: 41.9 us
  Pallas kernels  41.3 us (98%)
  local copies, waits for them, and re-layouts  0.61 us (1%)
    pallas_call x1, Pallas kernels, body(): pl.pallas_call(kernel, out_shape=pltpu.VMEM((8, factors), F32), in_specs=...  41.3 us

profile of v5, /device:TPU:1, one launch (start us, length us, event | category | flops | bytes accessed | tf_op | source)
XLA Modules:
  0.0 41.9 jit_solution(4131595447312117821)
XLA Ops:
  0.0 41.3 %shard_map.73 = f32[8,512]{1,0:T(8,128)S(1)} custom-call(bf16[128,16,512]{2,1,0:T(8,128)(2,1)} %normals.1, bf16[128,512]{1,0:T(8,128)(2,1)} %states.1, bf16[2048,512]{1,0:T(8,128)(2,1)} %loadings.1, f32[2048]{0:T(1024)} %strikes.1, f32[2048]{0:T(1024)} %hedge.1, f32[1,512]{1,0:T(1,128)} %bitcast.1, s32[256]{0:T(256)} %tail.1), custom_call_target="tpu_custom_call" | custom-call | tf_op jit(solution)/shard_map/pallas_call | solution.py:362
  41.3 0.6 %copy.9 = f32[8,512]{1,0:T(8,128)} copy(f32[8,512]{1,0:T(8,128)S(1)} %shard_map.73) | data formatting | bytes 32768

commit v6 on v5

--- a/solution.py
+++ b/solution.py
@@ -63,9 +63,6 @@
         greet((lax.rem(z + d, 8), me))
     partner = (z, device(0, 0, 1))
     greet(partner)
-    for item in loads[2:]:
-        item.start()
-
     loads[0].wait()
     first = jnp.int32(0)
     step = tails // 2
@@ -83,6 +80,8 @@
 
     lax.fori_loop(0, CAP, find, 0, unroll=8)
     loads[1].wait()
+    for item in loads[2:]:
+        item.start()
 
     def add_up(q, carry):
         for i in range(5):

time: 42 us -> 42 us (level)
  no operation moved by 1% of the time
where the time goes in v6:
time: 42 us; the launch traced here: 41.9 us
  Pallas kernels  41.3 us (98%)
  local copies, waits for them, and re-layouts  0.61 us (1%)
    pallas_call x1, Pallas kernels, body(): pl.pallas_call(kernel, out_shape=pltpu.VMEM((8, factors), F32), in_specs=...  41.3 us

profile of v6, /device:TPU:1, one launch (start us, length us, event | category | flops | bytes accessed | tf_op | source)
XLA Modules:
  0.0 41.9 jit_solution(11365416809801376186)
XLA Ops:
  0.0 41.3 %shard_map.73 = f32[8,512]{1,0:T(8,128)S(1)} custom-call(bf16[128,16,512]{2,1,0:T(8,128)(2,1)} %normals.1, bf16[128,512]{1,0:T(8,128)(2,1)} %states.1, bf16[2048,512]{1,0:T(8,128)(2,1)} %loadings.1, f32[2048]{0:T(1024)} %strikes.1, f32[2048]{0:T(1024)} %hedge.1, f32[1,512]{1,0:T(1,128)} %bitcast.1, s32[256]{0:T(256)} %tail.1), custom_call_target="tpu_custom_call" | custom-call | tf_op jit(solution)/shard_map/pallas_call | solution.py:361
  41.3 0.6 %copy.9 = f32[8,512]{1,0:T(8,128)} copy(f32[8,512]{1,0:T(8,128)S(1)} %shard_map.73) | data formatting | bytes 32768

commit v7 on v6

--- a/solution.py
+++ b/solution.py
@@ -98,19 +98,19 @@
         return carry
 
     lax.fori_loop(0, 16, add_up, 0)
-    pl.semaphore_wait(barrier, 23)
-
-    join = pltpu.make_async_remote_copy(
-        src_ref=sums.at[1 - c], dst_ref=sums_pair, send_sem=join_sem.at[0], recv_sem=join_sem.at[1],
-        device_id=partner, device_id_type=MESH,
-    )
-    join.start()
     for item in loads[2:]:
         item.wait()
     for b in range(4):
         lanes = slice(b * 128, b * 128 + 128)
         states_f[b] = states_b[:, lanes].astype(F32)
         sigma_f[b] = sigma_v[:, lanes]
+    pl.semaphore_wait(barrier, 23)
+
+    join = pltpu.make_async_remote_copy(
+        src_ref=sums.at[1 - c], dst_ref=sums_pair, send_sem=join_sem.at[0], recv_sem=join_sem.at[1],
+        device_id=partner, device_id_type=MESH,
+    )
+    join.start()
     join.wait_recv()
     sums_chip[...] = sums[c] + sums_pair[...]
 

time: 42 us -> 42.7 us (1.017)
  Pallas kernels: 41.3 us -> 42 us
    pallas_call x1, Pallas kernels: 41.3 us -> 42 us  [body(): pl.pallas_call(kernel, out_shape=pltpu.VMEM((8, factors), F32), in_specs=...]
where the time goes in v7:
time: 42.7 us; the launch traced here: 42.6 us
  Pallas kernels  42 us (98%)
  local copies, waits for them, and re-layouts  0.61 us (1%)
    pallas_call x1, Pallas kernels, body(): pl.pallas_call(kernel, out_shape=pltpu.VMEM((8, factors), F32), in_specs=...  42 us

profile of v7, /device:TPU:1, one launch (start us, length us, event | category | flops | bytes accessed | tf_op | source)
XLA Modules:
  0.0 42.6 jit_solution(8858809012874013672)
XLA Ops:
  0.0 42.0 %shard_map.73 = f32[8,512]{1,0:T(8,128)S(1)} custom-call(bf16[128,16,512]{2,1,0:T(8,128)(2,1)} %normals.1, bf16[128,512]{1,0:T(8,128)(2,1)} %states.1, bf16[2048,512]{1,0:T(8,128)(2,1)} %loadings.1, f32[2048]{0:T(1024)} %strikes.1, f32[2048]{0:T(1024)} %hedge.1, f32[1,512]{1,0:T(1,128)} %bitcast.1, s32[256]{0:T(256)} %tail.1), custom_call_target="tpu_custom_call" | custom-call | tf_op jit(solution)/shard_map/pallas_call | solution.py:361
  42.0 0.6 %copy.9 = f32[8,512]{1,0:T(8,128)} copy(f32[8,512]{1,0:T(8,128)S(1)} %shard_map.73) | data formatting | bytes 32768
